TPU v7x, 32 devices: a whole 2x2x4 slice. The times are simulated.
32 devices in a mesh: dp: 4 (over z), tp: 8 (over y, x, core).
Axes of the slice: x: 2, y: 2, z: 4, core: 2. Of those that a mesh axis runs over, the one named last changes fastest.
Arguments:
- x_in: bfloat16 [4, 2048, 2048], P('dp', 'tp'), parts along dimension 0
- cond_vec: bfloat16 [4, 2048], P('dp'), parts along dimension 0
- rope_cos: float32 [2048, 64], P('tp')
- rope_sin: float32 [2048, 64], P('tp')
- w_mod: bfloat16 [2, 2048, 6144], replicated
- b_mod: bfloat16 [2, 6144], replicated
- w_in: bfloat16 [2, 2048, 16, 896], P(None, None, 'tp')
- b_in: bfloat16 [2, 16, 896], P(None, 'tp')
- q_scale: bfloat16 [2, 128], replicated
- k_scale: bfloat16 [2, 128], replicated
- w_out: bfloat16 [2, 16, 640, 2048], P(None, 'tp')
- b_out: bfloat16 [2, 2048], replicated
- d_out: bfloat16 [4, 2048, 2048], P('dp', 'tp'), parts along dimension 0
Outputs:
- output 1: bfloat16 [4, 2048, 2048], P('dp', 'tp'), parts along dimension 0
- output 2: bfloat16 [4, 2048, 2048], P('dp', 'tp'), parts along dimension 0
- output 3: float32 [8, 2048, 6144], P('dp'), parts along dimension 0
- output 4: float32 [8, 6144], P('dp'), parts along dimension 0
- output 5: bfloat16 [8, 2048, 16, 896], P('dp', None, 'tp'), parts along dimension 0
- output 6: float32 [8, 16, 896], P('dp', 'tp'), parts along dimension 0
- output 7: float32 [8, 128], P('dp'), parts along dimension 0
- output 8: float32 [8, 128], P('dp'), parts along dimension 0
- output 9: bfloat16 [8, 16, 640, 2048], P('dp', 'tp'), parts along dimension 0
- output 10: float32 [8, 2048], P('dp'), parts along dimension 0
There are 4 independent parts. A program takes and returns all parts, laid end to end along the dimension named above; an argument that names none is the same for every part.
All inputs are finite; a program needn't handle non-finite values.
Results may differ from a plain program's by a relative error of at most 0.02.
Values are sent between devices in bfloat16 or wider.
A program may use at most 1 GiB of HBM per device.

v0:
```python
import functools
import jax
import jax.numpy as jnp
from jax import lax
from jax.sharding import PartitionSpec as P

NORM_EPS = 1e-6


def rms_norm(tensor):
    return tensor * lax.rsqrt(jnp.mean(tensor * tensor, axis=-1, keepdims=True) + NORM_EPS)


def apply_rope(tensor, rope_cos, rope_sin):
    pair_view = tensor.reshape(tensor.shape[:-1] + (tensor.shape[-1] // 2, 2))
    even_part = pair_view[..., 0]
    odd_part = pair_view[..., 1]
    cos_wide = rope_cos[None, :, None, :]
    sin_wide = rope_sin[None, :, None, :]
    rotated = jnp.stack([even_part * cos_wide - odd_part * sin_wide, even_part * sin_wide + odd_part * cos_wide], axis=-1)
    return rotated.reshape(tensor.shape)


def layer_modulate(x_f32, mod_shift, mod_scale):
    row_mean = jnp.mean(x_f32, axis=-1, keepdims=True)
    centered = x_f32 - row_mean
    row_var = jnp.mean(centered * centered, axis=-1, keepdims=True)
    normed = centered * lax.rsqrt(row_var + NORM_EPS)
    return (normed * (1.0 + mod_scale[:, None, :]) + mod_shift[:, None, :]).astype(jnp.bfloat16)


def mix_heads(projected, q_scale, k_scale, rope_cos, rope_sin):
    head_dim = q_scale.shape[-1]
    q_rot = apply_rope(rms_norm(projected[..., :head_dim]) * q_scale, rope_cos, rope_sin).astype(jnp.bfloat16)
    k_rot = apply_rope(rms_norm(projected[..., head_dim:2 * head_dim]) * k_scale, rope_cos, rope_sin).astype(jnp.bfloat16)
    v_part = projected[..., 2 * head_dim:3 * head_dim].astype(jnp.bfloat16)
    scores = jnp.einsum("bqhe,bkhe->bhqk", q_rot, k_rot, preferred_element_type=jnp.float32) * (head_dim ** -0.5)
    attn_probs = jax.nn.softmax(scores, axis=-1).astype(jnp.bfloat16)
    attn_out = jnp.einsum("bhqk,bkhe->bqhe", attn_probs, v_part, preferred_element_type=jnp.float32).astype(jnp.bfloat16)
    mlp_act = jax.nn.gelu(projected[..., 3 * head_dim:], approximate=True).astype(jnp.bfloat16)
    return jnp.concatenate([attn_out, mlp_act], axis=-1)


def solution(mesh):
    act_spec = P("dp", "tp", None)
    in_specs = (act_spec, P("dp", None), P("tp", None), P("tp", None), P(None, None, None), P(None, None), P(None, None, "tp", None), P(None, "tp", None), P(None, None), P(None, None), P(None, "tp", None, None), P(None, None), act_spec)
    out_specs = (act_spec, act_spec, P("dp", None, None), P("dp", None), P("dp", None, "tp", None), P("dp", "tp", None), P("dp", None), P("dp", None), P("dp", "tp", None, None), P("dp", None))

    def device_fn(x_in, cond_vec, rope_cos, rope_sin, w_mod, b_mod, w_in, b_in, q_scale, k_scale, w_out, b_out, d_out):
        num_blocks = w_in.shape[0]
        cos_full = lax.all_gather(rope_cos, "tp", axis=0, tiled=True)
        sin_full = lax.all_gather(rope_sin, "tp", axis=0, tiled=True)
        core_fn = functools.partial(mix_heads, rope_cos=cos_full, rope_sin=sin_full)
        silu_vec = jax.nn.silu(cond_vec.astype(jnp.float32)).astype(jnp.bfloat16)
        saved_acts = []
        x_cur = x_in
        for block_idx in range(num_blocks):
            mod_vec = jnp.dot(silu_vec, w_mod[block_idx], preferred_element_type=jnp.float32) + b_mod[block_idx].astype(jnp.float32)
            mod_shift, mod_scale, mod_gate = jnp.split(mod_vec, 3, axis=-1)
            x_f32 = x_cur.astype(jnp.float32)
            normed = layer_modulate(x_f32, mod_shift, mod_scale)
            normed_full = lax.all_gather(normed, "tp", axis=1, tiled=True)
            projected = jnp.einsum("bsd,dhc->bshc", normed_full, w_in[block_idx], preferred_element_type=jnp.float32) + b_in[block_idx].astype(jnp.float32)
            joined = core_fn(projected, q_scale[block_idx].astype(jnp.float32), k_scale[block_idx].astype(jnp.float32))
            part_out = jnp.einsum("bshc,hcd->bsd", joined, w_out[block_idx], preferred_element_type=jnp.float32)
            mixed_out = lax.psum_scatter(part_out.astype(jnp.bfloat16), "tp", scatter_dimension=1, tiled=True)
            branch = mixed_out.astype(jnp.float32) + b_out[block_idx].astype(jnp.float32)
            saved_acts.append((x_f32, mod_vec, normed_full, projected, joined, branch))
            x_cur = (x_f32 + mod_gate[:, None, :] * branch).astype(jnp.bfloat16)
        x_out = x_cur

        silu_f32 = silu_vec.astype(jnp.float32)
        grad_cur = d_out
        block_grads = {}
        for block_idx in reversed(range(num_blocks)):
            x_f32, mod_vec, normed_full, projected, joined, branch = saved_acts[block_idx]
            mod_shift, mod_scale, mod_gate = jnp.split(mod_vec, 3, axis=-1)
            qs_f32 = q_scale[block_idx].astype(jnp.float32)
            ks_f32 = k_scale[block_idx].astype(jnp.float32)
            grad_f32 = grad_cur.astype(jnp.float32)
            d_gate = jnp.sum(grad_f32 * branch, axis=1)
            gated_grad = grad_f32 * mod_gate[:, None, :]
            d_bout = lax.psum(jnp.sum(gated_grad, axis=(0, 1)), "tp")
            d_branch = lax.all_gather(gated_grad.astype(jnp.bfloat16), "tp", axis=1, tiled=True)
            g_wout = jnp.einsum("bshc,bsd->hcd", joined, d_branch, preferred_element_type=jnp.float32).astype(jnp.bfloat16)
            d_joined = jnp.einsum("bsd,hcd->bshc", d_branch, w_out[block_idx], preferred_element_type=jnp.float32).astype(jnp.bfloat16)
            unused_out, core_pull = jax.vjp(core_fn, projected, qs_f32, ks_f32)
            d_proj, d_qs, d_ks = core_pull(d_joined)
            g_bin = jnp.sum(d_proj, axis=(0, 1))
            d_proj16 = d_proj.astype(jnp.bfloat16)
            g_win = jnp.einsum("bsd,bshc->dhc", normed_full, d_proj16, preferred_element_type=jnp.float32).astype(jnp.bfloat16)
            d_norm_part = jnp.einsum("bshc,dhc->bsd", d_proj16, w_in[block_idx], preferred_element_type=jnp.float32)
            d_normed = lax.psum_scatter(d_norm_part.astype(jnp.bfloat16), "tp", scatter_dimension=1, tiled=True)
            unused_norm, norm_pull = jax.vjp(layer_modulate, x_f32, mod_shift, mod_scale)
            d_xnorm, d_shift, d_scale = norm_pull(d_normed)
            d_mod = lax.psum(jnp.concatenate([d_shift, d_scale, d_gate], axis=-1), "tp")
            g_wmod = jnp.einsum("bd,bm->dm", silu_f32, d_mod, preferred_element_type=jnp.float32)
            block_grads[block_idx] = (g_wmod, jnp.sum(d_mod, axis=0), g_win, g_bin, lax.psum(d_qs, "tp"), lax.psum(d_ks, "tp"), g_wout, d_bout)
            grad_cur = (grad_f32 + d_xnorm).astype(jnp.bfloat16)
        stacked = tuple(jnp.stack([block_grads[block_idx][entry_idx] for block_idx in range(num_blocks)]) for entry_idx in range(8))
        return (x_out, grad_cur) + stacked

    return jax.shard_map(device_fn, mesh=mesh, in_specs=in_specs, out_specs=out_specs, check_vma=False)
```

profile of v0, /device:TPU:0, one launch (start us, length us, event | category | flops | bytes accessed | tf_op | source)
XLA Modules:
  0.0 1262.7 jit_solution(252297172526843031)
XLA Ops:
  36.7 18.8 %copy.145 = bf16[1,2048,2,896]{1,3,2,0:T(8,128)(2,1)} copy(bf16[1,2048,2,896]{3,2,1,0:T(2,128)(2,1)} %get-tuple-element.80) | data formatting | bytes 14680064
  84.9 20.1 %add_bitcast_fusion.1 = f32[1,2048,2,896]{1,3,2,0:T(8,128)S(1)} fusion(f32[2,896]{1,0:T(2,128)S(1)} %get-tuple-element.124, bf16[1,2048,2,896]{1,3,2,0:T(8,128)(2,1)} %copy.145, bf16[1,2048,2048]{2,1,0:T(8,128)(2,1)} %all-gather.5.cloned.1.call-done), kind=kOutput, calls=%fused_computation.43 | convolution fusion | flops 15036055552 | bytes 30415872 | tf_op jit(solution)/shard_map/bsd,dhc->bshc/dot_general | solution.py:63
  121.9 19.8 %fusion.235 = (f32[2,2048]{1,0:T(2,128)S(1)}, f32[2,2048,2048]{1,2,0:T(8,128)}) fusion(bf16[2048,2,128]{0,1,2:T(2,128)(2,1)} %bitcast.327, bf16[2048,2,128]{0,1,2:T(2,128)(2,1)S(1)} %bitcast.325), kind=kOutput, calls=%fused_computation.331 | convolution fusion | flops 2172651520 | bytes 35667968 | tf_op jit(solution)/shard_map/sub | solution.py:38
  194.3 57.5 %reduce-scatter.5.cloned.1.call-done = bf16[1,256,2048]{2,1,0:T(8,128)(2,1)} async-done(((bf16[1,2048,2048]{2,1,0:T(8,128)(2,1)}), bf16[1,256,2048]{2,1,0:T(8,128)(2,1)}) %reduce-scatter.5.cloned.1.call-update) | async-done | bytes 1048592 | tf_op jit(solution)/shard_map/reduce_scatter | solution.py:66
  256.1 18.7 %copy.146 = bf16[1,2048,2,896]{1,3,2,0:T(8,128)(2,1)} copy(bf16[1,2048,2,896]{3,2,1,0:T(2,128)(2,1)} %get-tuple-element.79) | data formatting | bytes 14680064
  274.9 32.8 %all-gather.9.cloned.1.call-done = bf16[1,2048,2048]{2,1,0:T(8,128)(2,1)} async-done(((bf16[1,256,2048]{2,1,0:T(8,128)(2,1)}), bf16[1,2048,2048]{2,1,0:T(8,128)(2,1)}) %all-gather.9.cloned.1.call-update) | async-done | bytes 8388624 | tf_op jit(solution)/shard_map/all_gather | solution.py:84
  324.2 39.6 %all-gather.7.cloned.1.call-done = bf16[1,2048,2048]{2,1,0:T(8,128)(2,1)} async-done(((bf16[1,256,2048]{2,1,0:T(8,128)(2,1)}), bf16[1,2048,2048]{2,1,0:T(8,128)(2,1)}) %all-gather.7.cloned.1.call-update) | async-done | bytes 8388624 | tf_op jit(solution)/shard_map/all_gather | solution.py:62
  363.9 20.5 %add_bitcast_fusion = f32[1,2048,2,896]{1,3,2,0:T(8,128)S(1)} fusion(f32[2,896]{1,0:T(2,128)S(1)} %get-tuple-element.123, bf16[1,2048,2,896]{1,3,2,0:T(8,128)(2,1)} %copy.146, bf16[1,2048,2048]{2,1,0:T(8,128)(2,1)} %all-gather.7.cloned.1.call-done), kind=kOutput, calls=%fused_computation.42 | convolution fusion | flops 15036055552 | bytes 30415872 | tf_op jit(solution)/shard_map/bsd,dhc->bshc/dot_general | solution.py:63
  421.4 22.7 %fusion.6 = (f32[2,2048]{1,0:T(2,128)S(1)}, bf16[2,2048,2048]{1,2,0:T(8,128)(2,1)}, bf16[2,2048,2048]{1,2,0:T(8,128)(2,1)}) fusion(f32[2,2048,2048]{1,2,0:T(8,128)} %get-tuple-element.132, f32[2,2048]{1,0:T(2,128)S(1)} %multiply_divide_fusion.1, f32[2,2048]{1,0:T(2,128)S(1)} %get-tuple-element.131, f32[1,2048,2,896]{1,3,2,0:T(8,128)} %copy-done.3, ...), kind=kOutput, calls=%fused_computation.13 | convolution fusion | flops 2206199808 | bytes 69255168 | tf_op jit(solution)/shard_map/transpose(jvp(bhqk,bkhe->bqhe))/dot_general | solution.py:39
  444.1 17.6 %fusion.143 = f32[1,2048,2,128]{1,3,2,0:T(8,128)S(1)} fusion(bf16[2048,2,128]{0,1,2:T(2,128)(2,1)S(1)} %bitcast.332, f32[2,2048,2048]{1,2,0:T(8,128)} %get-tuple-element.132, bf16[2,2048,2048]{1,2,0:T(8,128)(2,1)} %get-tuple-element.133, f32[2,2048]{1,0:T(2,128)S(1)} %neg.49, f32[2,2048]{1,0:T(2,128)S(1)} %get-tuple-element.131), kind=kOutput, calls=%fused_computation.176 | convolution fusion | flops 2190475264 | bytes 53510144 | tf_op jit(solution)/shard_map/transpose(jvp(bqhe,bkhe->bhqk))/dot_general | solution.py:37
  461.7 19.3 %fusion.140 = f32[1,2048,2,128]{1,3,2,0:T(8,128)} fusion(bf16[2048,2,128]{0,1,2:T(2,128)(2,1)S(1)} %bitcast.330, f32[2,2048,2048]{1,2,0:T(8,128)} %get-tuple-element.132, bf16[2,2048,2048]{1,2,0:T(8,128)(2,1)} %get-tuple-element.133, f32[2,2048]{1,0:T(2,128)S(1)} %neg.49, f32[2,2048]{1,0:T(2,128)S(1)} %get-tuple-element.131), kind=kOutput, calls=%fused_computation.173 | convolution fusion | flops 2190475264 | bytes 53510144 | tf_op jit(solution)/shard_map/transpose(jvp(bqhe,bkhe->bhqk))/dot_general | solution.py:37
  514.8 23.1 %fusion.74 = bf16[1,2048,2048]{2,1,0:T(8,128)(2,1)} fusion(bf16[1,2048,2,896]{1,3,2,0:T(8,128)(2,1)} %copy.146, f32[1,2048,2,128]{1,3,2,0:T(8,128)} %get-tuple-element.76, f32[1,2048,2,128]{1,3,2,0:T(8,128)S(1)} %get-tuple-element.75, bf16[1,2048,2,128]{1,3,2,0:T(8,128)(2,1)S(1)} %fusion.152, f32[1,2048,2,512]{1,3,2,0:T(8,128)} %get-tuple-element.73), kind=kOutput, calls=%fused_computation.107 | convolution fusion | flops 15054929920 | bytes 29360128 | tf_op jit(solution)/shard_map/bshc,dhc->bsd/dot_general | solution.py:92
  564.0 44.7 %reduce-scatter.9.cloned.1.call-done = bf16[1,256,2048]{2,1,0:T(8,128)(2,1)} async-done(((bf16[1,2048,2048]{2,1,0:T(8,128)(2,1)}), bf16[1,256,2048]{2,1,0:T(8,128)(2,1)}) %reduce-scatter.9.cloned.1.call-update) | async-done | bytes 1048592 | tf_op jit(solution)/shard_map/reduce_scatter | solution.py:93
  614.1 68.5 %reduce-scatter.7.cloned.1.call-done = bf16[1,256,2048]{2,1,0:T(8,128)(2,1)} async-done(((bf16[1,2048,2048]{2,1,0:T(8,128)(2,1)}), bf16[1,256,2048]{2,1,0:T(8,128)(2,1)}) %reduce-scatter.7.cloned.1.call-update) | async-done | bytes 1048592 | tf_op jit(solution)/shard_map/reduce_scatter | solution.py:66
  691.2 25.1 %convert_bitcast_fusion = bf16[1,2048,2,896]{3,1,2,0:T(8,128)(2,1)} fusion(bf16[1,2048,2048]{2,1,0:T(8,128)(2,1)} %all-gather.7.cloned.1.call-done, f32[1,2048,2,128]{1,3,2,0:T(8,128)} %get-tuple-element.76, f32[1,2048,2,128]{1,3,2,0:T(8,128)S(1)} %get-tuple-element.75, bf16[1,2048,2,128]{1,3,2,0:T(8,128)(2,1)} %copy-done.26, ...), kind=kOutput, calls=%fused_computation.99 | convolution fusion | flops 15054405632 | bytes 29360128 | tf_op jit(solution)/shard_map/bsd,bshc->dhc/dot_general | solution.py:91
  716.3 27.6 %all-gather.11.cloned.1.call-done = bf16[1,2048,2048]{2,1,0:T(8,128)(2,1)} async-done(((bf16[1,256,2048]{2,1,0:T(8,128)(2,1)}), bf16[1,2048,2048]{2,1,0:T(8,128)(2,1)}) %all-gather.11.cloned.1.call-update) | async-done | bytes 8388624 | tf_op jit(solution)/shard_map/all_gather | solution.py:84
  744.0 16.9 %convert_bitcast_fusion.4 = bf16[1,2048,2,640]{1,3,2,0:T(8,128)(2,1)} fusion(bf16[2,2,640,2048]{3,2,1,0:T(8,128)(2,1)} %param.23, bf16[1,2048,2048]{2,1,0:T(8,128)(2,1)} %all-gather.11.cloned.1.call-done), kind=kOutput, calls=%fused_computation.117 | convolution fusion | flops 10740039680 | bytes 18874368 | tf_op jit(solution)/shard_map/bsd,hcd->bshc/dot_general | solution.py:86
  849.0 23.2 %fusion.79 = bf16[1,2048,2048]{2,1,0:T(8,128)(2,1)} fusion(bf16[1,2048,2,896]{1,3,2,0:T(8,128)(2,1)} %copy.145, f32[1,2048,2,128]{1,3,2,0:T(8,128)} %get-tuple-element.72, f32[1,2048,2,128]{1,3,2,0:T(8,128)S(1)} %get-tuple-element.71, bf16[1,2048,2,128]{1,3,2,0:T(8,128)(2,1)S(1)} %copy-done.28, f32[1,2048,2,512]{1,3,2,0:T(8,128)} %fusion.31), kind=kOutput, calls=%fused_computation.108 | convolution fusion | flops 15054929920 | bytes 29360128 | tf_op jit(solution)/shard_map/bshc,dhc->bsd/dot_general | solution.py:92
  872.3 16.6 %convert_bitcast_fusion.2 = bf16[1,2,640,2048]{3,2,1,0:T(8,128)(2,1)} fusion(bf16[1,2048,2048]{2,1,0:T(8,128)(2,1)} %all-gather.9.cloned.1.call-done, bf16[1,2048,2,512]{1,3,2,0:T(8,128)(2,1)} %get-tuple-element.74, bf16[1,2048,2,128]{1,3,2,0:T(8,128)(2,1)} %copy-done.32), kind=kOutput, calls=%fused_computation.115 | convolution fusion | flops 10750525440 | bytes 18874368 | tf_op jit(solution)/shard_map/bshc,bsd->hcd/dot_general | solution.py:85
  894.1 25.4 %convert_bitcast_fusion.1 = bf16[1,2048,2,896]{3,1,2,0:T(8,128)(2,1)} fusion(bf16[1,2048,2048]{2,1,0:T(8,128)(2,1)} %all-gather.5.cloned.1.call-done, f32[1,2048,2,128]{1,3,2,0:T(8,128)} %get-tuple-element.72, f32[1,2048,2,128]{1,3,2,0:T(8,128)} %copy-done.19, bf16[1,2048,2,128]{1,3,2,0:T(8,128)(2,1)} %fusion.153, f32[1,2048,2,512]{1,3,2,0:T(8,128)} %fusion.31), kind=kOutput, calls=%fused_computation.100 | convolution fusion | flops 15054405632 | bytes 29360128 | tf_op jit(solution)/shard_map/bsd,bshc->dhc/dot_general | solution.py:91
  927.6 137.8 %copy.108 = bf16[2,2048,2,896]{3,2,1,0:T(2,128)(2,1)} copy(bf16[2,2048,2,896]{3,1,2,0:T(8,128)(2,1)S(1)} %pad_maximum_fusion.1) | data formatting | bytes 29360128
  1100.4 52.3 %all-reduce.19.cloned.1.call-done = (f32[1,6144]{1,0:T(1,128)}, f32[1,6144]{1,0:T(1,128)}, f32[1,128]{1,0:T(1,128)}, f32[1,128]{1,0:T(1,128)}, f32[1,128]{1,0:T(...) async-done(((f32[1,6144]{1,0:T(1,128)}, f32[1,6144]{1,0:T(1,128)}, f32[1,128]{1,0:T(1,128)}, f32[1,128]{1,0:T(1,128)}, f32[1,128]{1,0:T(1,128)}, ...) | async-done | bytes 67600 | tf_op jit(solution)/shard_map/psum | solution.py:96
  1157.9 32.8 %multiply_bitcast_fusion.1 = (f32[1,2048,6144]{2,1,0:T(8,128)}, f32[1,2048,6144]{2,1,0:T(8,128)}) fusion(f32[6144]{0:T(1024)} %bitcast.345, f32[2048]{0:T(1024)S(1)} %copy-done.75, f32[6144]{0:T(1024)} %bitcast.344), kind=kLoop, calls=%fused_computation.4 | loop fusion | flops 25165824 | bytes 100720640 | tf_op jit(solution)/shard_map/stack | solution.py:100
  1190.7 65.2 %pad_maximum_fusion = f32[2,2048,6144]{2,1,0:T(8,128)} fusion(f32[1,2048,6144]{2,1,0:T(8,128)} %get-tuple-element.120, f32[1,2048,6144]{2,1,0:T(8,128)} %get-tuple-element.119), kind=kLoop, calls=%fused_computation.2 | loop fusion | flops 25165824 | bytes 201326592 | tf_op jit(solution)/shard_map/stack | solution.py:100
  (336 shorter events, 400.5 us)
Async XLA Ops:
  7.2 77.7 %all-gather.5.cloned.1.call-start = ((), (), s32[]{:S(2)}) async-start(), calls=%async_computation.4 | async-start | bytes 9437184 | tf_op jit(solution)/shard_map/all_gather | solution.py:62
  21.8 230.0 %copy-start.58 = (f32[1,2048]{1,0:T(1,128)}, f32[1,2048]{1,0:T(1,128)S(1)}, u32[]{:S(2)}) copy-start(f32[1,2048]{1,0:T(1,128)S(1)} %get-tuple-element.116) | copy-start | bytes 24580
  23.9 228.0 %reduce-scatter.5.cloned.1.call-start = ((), (), s32[]{:S(2)}) async-start(), calls=%async_computation.5 | async-start | bytes 9437184 | tf_op jit(solution)/shard_map/reduce_scatter | solution.py:66
  69.4 330.7 %copy-start.8 = (f32[2048,64]{0,1:T(8,128)}, f32[2048,64]{0,1:T(8,128)S(1)}, u32[]{:S(2)}) copy-start(f32[2048,64]{0,1:T(8,128)S(1)} %all_gather.19) | copy-start | bytes 1572868
  81.9 318.2 %copy-start.11 = (f32[2048,64]{0,1:T(8,128)}, f32[2048,64]{0,1:T(8,128)S(1)}, u32[]{:S(2)}) copy-start(f32[2048,64]{0,1:T(8,128)S(1)} %all_gather.20) | copy-start | bytes 1572868
  181.1 126.6 %all-gather.9.cloned.1.call-start = ((), (), s32[]{:S(2)}) async-start(), calls=%async_computation.8 | async-start | bytes 9437184 | tf_op jit(solution)/shard_map/all_gather | solution.py:84
  193.7 170.2 %all-gather.7.cloned.1.call-start = ((), (), s32[]{:S(2)}) async-start(), calls=%async_computation.6 | async-start | bytes 9437184 | tf_op jit(solution)/shard_map/all_gather | solution.py:62
  256.1 352.6 %reduce-scatter.9.cloned.1.call-start = ((), (), s32[]{:S(2)}) async-start(), calls=%async_computation.9 | async-start | bytes 9437184 | tf_op jit(solution)/shard_map/reduce_scatter | solution.py:93
  514.8 176.4 %copy-start.16 = (f32[1,2048,2,128]{1,3,2,0:T(8,128)}, f32[1,2048,2,128]{1,3,2,0:T(8,128)S(1)}, u32[]{:S(2)}) copy-start(f32[1,2048,2,128]{1,3,2,0:T(8,128)S(1)} %get-tuple-element.75) | copy-start | bytes 6291460
  538.0 144.7 %reduce-scatter.7.cloned.1.call-start = ((), (), s32[]{:S(2)}) async-start(), calls=%async_computation.7 | async-start | bytes 9437184 | tf_op jit(solution)/shard_map/reduce_scatter | solution.py:66
  563.9 118.7 %copy-start.59 = (f32[1,2048]{1,0:T(1,128)S(1)}, f32[1,2048]{1,0:T(1,128)}, u32[]{:S(2)}) copy-start(f32[1,2048]{1,0:T(1,128)} %copy-done.58) | copy-start | bytes 24580
  563.9 118.7 %copy-start.63 = (f32[1,2048]{1,0:T(1,128)S(1)}, f32[1,2048]{1,0:T(1,128)}, u32[]{:S(2)}) copy-start(f32[1,2048]{1,0:T(1,128)} %copy-done.62) | copy-start | bytes 24580
  563.9 118.7 %copy-start.65 = (f32[1,2048]{1,0:T(1,128)S(1)}, f32[1,2048]{1,0:T(1,128)}, u32[]{:S(2)}) copy-start(f32[1,2048]{1,0:T(1,128)} %copy-done.64) | copy-start | bytes 24580
  563.9 118.7 %copy-start.79 = (f32[1,2048]{1,0:T(1,128)S(1)}, f32[1,2048]{1,0:T(1,128)}, u32[]{:S(2)}) copy-start(f32[1,2048]{1,0:T(1,128)} %get-tuple-element.121) | copy-start | bytes 24580
  563.9 126.0 %copy-start.61 = (bf16[1,2048]{1,0:T(2,128)(2,1)S(1)}, bf16[1,2048]{1,0:T(2,128)(2,1)}, u32[]{:S(2)}) copy-start(bf16[1,2048]{1,0:T(2,128)(2,1)} %param.14) | copy-start | bytes 12292
  564.0 126.6 %copy-start.67 = (f32[2,2048]{1,0:T(2,128)S(1)}, f32[2,2048]{1,0:T(2,128)}, u32[]{:S(2)}) copy-start(f32[2,2048]{1,0:T(2,128)} %copy-done.66) | copy-start | bytes 49156
  564.0 180.0 %all-gather.11.cloned.1.call-start = ((), (), s32[]{:S(2)}) async-start(), calls=%async_computation.10 | async-start | bytes 9437184 | tf_op jit(solution)/shard_map/all_gather | solution.py:84
  689.9 402.5 %reduce-scatter.11.cloned.1.call-start = ((), (), s32[]{:S(2)}) async-start(), calls=%async_computation.11 | async-start | bytes 9437184 | tf_op jit(solution)/shard_map/reduce_scatter | solution.py:93
  872.3 280.5 %all-reduce.19.cloned.1.call-start = ((), (), s32[]{:S(2)}) async-start(), calls=%async_computation.12 | async-start | bytes 135168 | tf_op jit(solution)/shard_map/psum | solution.py:96
  919.5 145.9 %slice-start = ((s8[8388608]{0:T(1024)(128)(4,1)}), s8[4194304]{0:T(1024)(128)(4,1)S(1)}, s32[]{:S(2)}) async-start(s8[8388608]{0:T(1024)(128)(4,1)} %bitcast.305), calls=%async_computation.13 | async-start | bytes 8388608
  927.6 137.8 %slice-start.1 = ((s8[8388608]{0:T(1024)(128)(4,1)}), s8[4194304]{0:T(1024)(128)(4,1)S(1)}, s32[]{:S(2)}) async-start(s8[8388608]{0:T(1024)(128)(4,1)} %bitcast.305), calls=%async_computation.14 | async-start | bytes 8388608
  927.6 137.8 %copy-start.20 = (f32[1,2048,2,128]{1,3,2,0:T(8,128)S(1)}, f32[1,2048,2,128]{1,3,2,0:T(8,128)}, u32[]{:S(2)}) copy-start(f32[1,2048,2,128]{1,3,2,0:T(8,128)} %copy-done.19) | copy-start | bytes 6291460
  927.6 137.8 %copy-start.21 = (f32[1,2048,2,128]{1,3,2,0:T(8,128)S(1)}, f32[1,2048,2,128]{1,3,2,0:T(8,128)}, u32[]{:S(2)}) copy-start(f32[1,2048,2,128]{1,3,2,0:T(8,128)} %get-tuple-element.72) | copy-start | bytes 6291460
  927.6 137.8 %copy-start.29 = (bf16[1,2048,2,128]{1,3,2,0:T(8,128)(2,1)S(1)}, bf16[1,2048,2,128]{1,3,2,0:T(8,128)(2,1)}, u32[]{:S(2)}) copy-start(bf16[1,2048,2,128]{1,3,2,0:T(8,128)(2,1)} %fusion.153) | copy-start | bytes 3145732
  (90 other events, 1356.1 us)
Sparse Core Ops, SparseCore 0:
  24.0 60.8 all-gather.4
  181.2 70.6 reduce-scatter.4
  253.7 53.8 all-gather.8
  310.0 53.8 all-gather.6
  538.1 70.5 reduce-scatter.8
  612.0 70.5 reduce-scatter.6
  690.0 53.8 all-gather.10
  872.4 70.5 reduce-scatter.10
  1097.4 55.2 all-reduce.18
where the time goes:
time: 1270 us; the launch traced here: 1260 us
  matrix products  431 us (34%)
  waiting for transfers between devices  325 us (26%)
  other arithmetic  239 us (19%)
  local copies, waits for them, and re-layouts  224 us (18%)
  blocking collectives  26.4 us (2%)
  between operations  15.5 us (1%)
    unnamed x213, local copies, waits for them, and re-layouts  193 us
    reduce_scatter x2, waiting for transfers between devices, device_fn(): lax.psum_scatter(part_out.astype(jnp.bfloat16), 'tp', scatter_dimension=1...  126 us
    another operation x9, other arithmetic, device_fn(): jnp.stack([block_grads[block_idx][entry_idx] for block_idx in range(num_b...  121 us
    dot_general x6, matrix products, mix_heads(): jnp.einsum('bhqk,bkhe->bqhe', attn_probs, v_part, preferred_element_type=...  74.2 us
    dot_general x4, matrix products, mix_heads(): jnp.einsum('bqhe,bkhe->bhqk', q_rot, k_rot, preferred_element_type=jnp.fl...  67 us
    all_gather x2, waiting for transfers between devices, device_fn(): lax.all_gather(gated_grad.astype(jnp.bfloat16), 'tp', axis=1, tiled=True)  60.4 us
    psum x1, waiting for transfers between devices, device_fn(): d_mod = lax.psum(jnp.concatenate([d_shift, d_scale, d_gate], axis=-1), 'tp')  52.3 us
    dot_general x2, matrix products, device_fn(): jnp.einsum('bsd,bshc->dhc', normed_full, d_proj16, preferred_element_type...  50.5 us
  transfers between devices with their start and end apart: 9, of which 8 were waited for; matrix products, arithmetic and copies ran while one was open for 29% of the time, Pallas kernels for 0%

commit v1 on v0

v1 whole, which is shorter than its diff:
```python
import functools
import jax
import jax.numpy as jnp
from jax import lax
from jax.experimental import pallas as pl
from jax.experimental.pallas import tpu as pltpu
from jax.sharding import PartitionSpec as P

EPS = 1e-6
MESH = pl.DeviceIdType.MESH
ANY = pl.BlockSpec(memory_space=pl.ANY)
VM = pl.BlockSpec(memory_space=pltpu.VMEM)
F32 = jnp.float32
BF16 = jnp.bfloat16
LOG2E = 1.4426950408889634
VMEM_LIMIT = 62 * 1024 * 1024


def dot(a, b, dims=((1,), (0,)), precision=None):
    return lax.dot_general(a, b, (dims, ((), ())), preferred_element_type=F32, precision=precision)


def neighbours():
    me = lax.axis_index("tp")
    core = lax.rem(me, 2)
    xbit = lax.rem(lax.div(me, 2), 2)
    ybit = lax.div(me, 4)
    return {"p": me + 1 - 2 * core, "x": me + 2 - 4 * xbit, "y": me + 4 - 8 * ybit}


def slot_owner(slot):
    me = lax.axis_index("tp")
    out = me
    for bit in range(3):
        if (slot >> bit) & 1:
            mine = lax.rem(lax.div(me, 1 << bit), 2)
            out = out + (1 << bit) - (2 << bit) * mine
    return out


def barrier(nbrs):
    sem = pltpu.get_barrier_semaphore()
    for key in ("p", "x", "y"):
        pl.semaphore_signal(sem, inc=1, device_id={"tp": nbrs[key]}, device_id_type=MESH)
    pl.semaphore_wait(sem, 3)


class Gather:
    def __init__(self, buf, send, recv, nbrs, chunks):
        self.buf, self.send, self.recv, self.nbrs, self.chunks = buf, send, recv, nbrs, chunks
        self.rows = buf.shape[1] // chunks
        self.index = {}
        for ch in range(chunks):
            for key in (("y", 0, 4), ("x", 0, 2), ("p", 0, 1), ("p", 2, 3), ("p", 4, 5), ("p", 6, 7)):
                self.index[key + (ch,)] = len(self.index)
            key = ("y", 2, 6) if self.via_x(ch) else ("x", 4, 6)
            self.index[key + (ch,)] = len(self.index)

    def via_x(self, ch):
        return ch < (self.chunks + 1) // 2

    def copy(self, to, src, dst, ch):
        rows = pl.ds(ch * self.rows, self.rows)
        return pltpu.make_async_remote_copy(
            src_ref=self.buf.at[src, rows],
            dst_ref=self.buf.at[dst, rows],
            send_sem=self.send.at[self.index[(to, src, dst, ch)]],
            recv_sem=self.recv.at[dst * self.chunks + ch],
            device_id={"tp": self.nbrs[to]},
            device_id_type=MESH,
        )

    def start_own(self):
        for ch in range(self.chunks):
            self.copy("y", 0, 4, ch).start()
            self.copy("x", 0, 2, ch).start()
        for ch in range(self.chunks):
            self.copy("p", 0, 1, ch).start()

    def arrived(self, slot, ch):
        to, src = {1: ("p", 0), 2: ("x", 0), 3: ("p", 2), 4: ("y", 0), 5: ("p", 4), 7: ("p", 6)}.get(slot, (None, None))
        if slot == 6:
            to, src = ("y", 2) if self.via_x(ch) else ("x", 4)
        self.copy(to, src, slot, ch).wait_recv()

    def wait_slot(self, slot):
        for ch in range(self.chunks):
            self.arrived(slot, ch)

    def pass_neighbours(self):
        order = []
        half = (self.chunks + 1) // 2
        for ch in range(self.chunks):
            order.append((2, ch))
            order.append((4, ch))
        for slot, ch in order:
            self.arrived(slot, ch)
            if slot == 2 and self.via_x(ch):
                self.copy("y", 2, 6, ch).start()
            if slot == 4 and not self.via_x(ch):
                self.copy("x", 4, 6, ch).start()
            self.copy("p", slot, slot + 1, ch).start()

    def pass_diagonal(self):
        half = (self.chunks + 1) // 2
        for k in range(half):
            for ch in (k, k + half):
                if ch < self.chunks:
                    self.arrived(6, ch)
                    self.copy("p", 6, 7, ch).start()

    def before(self, step):
        @pl.when(step == 1)
        def _():
            self.wait_slot(1)

        @pl.when(step == 2)
        def _():
            self.pass_neighbours()

        @pl.when(step == 3)
        def _():
            self.wait_slot(3)

        @pl.when(step == 5)
        def _():
            self.wait_slot(5)

        @pl.when(step == 6)
        def _():
            self.pass_diagonal()

        @pl.when(step == 7)
        def _():
            self.wait_slot(7)

    def all_now(self):
        self.start_own()
        self.pass_neighbours()
        self.pass_diagonal()
        for slot in (1, 3, 5, 7):
            self.wait_slot(slot)

    def finish(self):
        for key in self.index:
            self.copy(*key).wait_send()


def gather_sems(chunks):
    return [pltpu.SemaphoreType.DMA((7 * chunks,)), pltpu.SemaphoreType.DMA((8 * chunks,))]


class Reduce:
    SENDS = ("p3", "p2", "p1", "p0", "xd", "yd", "yb", "ya", "xa", "xb")

    def __init__(self, part, pout, pin, dsum, ysum, xsum, xin, yin, ownx, owny, ykeep, xkeep, send, recv, nbrs):
        self.part, self.pout, self.pin = part, pout, pin
        self.dsum, self.ysum, self.xsum = dsum, ysum, xsum
        self.xin, self.yin, self.ownx, self.owny = xin, yin, ownx, owny
        self.ykeep, self.xkeep = ykeep, xkeep
        self.send, self.recv, self.nbrs = send, recv, nbrs
        self.half = part.shape[0] // 2

    def copy(self, key):
        lo, hi = pl.ds(0, self.half), pl.ds(self.half, self.half)
        src, dst, to = {
            "p3": (self.pout.at[3], self.pin.at[3], "p"),
            "p2": (self.pout.at[2], self.pin.at[2], "p"),
            "p1": (self.pout.at[1], self.pin.at[1], "p"),
            "p0": (self.pout.at[0], self.pin.at[0], "p"),
            "xd": (self.dsum.at[lo], self.xin, "x"),
            "yd": (self.dsum.at[hi], self.yin, "y"),
            "yb": (self.ysum.at[hi], self.owny.at[hi], "y"),
            "ya": (self.ysum.at[lo], self.owny.at[lo], "y"),
            "xa": (self.xsum.at[lo], self.ownx.at[lo], "x"),
            "xb": (self.xsum.at[hi], self.ownx.at[hi], "x"),
        }[key]
        i = self.SENDS.index(key)
        return pltpu.make_async_remote_copy(
            src_ref=src, dst_ref=dst, send_sem=self.send.at[i], recv_sem=self.recv.at[i],
            device_id={"tp": self.nbrs[to]}, device_id_type=MESH,
        )

    def rows_loop(self, start, count, body, step=16):
        def one(i, carry):
            body(pl.ds(pl.multiple_of(start + i * step, step), step), pl.ds(pl.multiple_of(i * step, step), step))
            return carry
        lax.fori_loop(0, count // step, one, 0)

    def after(self, step):
        half, full = self.half, 2 * self.half
        part, pin = self.part, self.pin

        for z in (3, 2, 1, 0):
            @pl.when(step == 6 - 2 * z)
            def _(z=z):
                def body(rows, unused):
                    self.pout[z, rows, :] = part[rows, :].astype(BF16)
                self.rows_loop(0, full, body)
                self.copy(f"p{z}").start()

        @pl.when(step == 1)
        def _():
            self.copy("p3").wait_recv()
            def body(rows, unused):
                self.dsum[rows, :] = (part[rows, :] + pin[3, rows, :].astype(F32)).astype(BF16)
            self.rows_loop(0, half, body)
            self.copy("xd").start()
            self.rows_loop(half, half, body)
            self.copy("yd").start()

        @pl.when(step == 3)
        def _():
            self.copy("p2").wait_recv()
            def body(rows, unused):
                self.ysum[rows, :] = (part[rows, :] + pin[2, rows, :].astype(F32)).astype(BF16)
            self.rows_loop(half, half, body)
            self.copy("yb").start()
            def keep(rows, base):
                self.ykeep[base, :] = part[rows, :] + pin[2, rows, :].astype(F32)
            self.rows_loop(0, half, keep)

        @pl.when(step == 5)
        def _():
            self.copy("p1").wait_recv()
            def body(rows, unused):
                self.xsum[rows, :] = (part[rows, :] + pin[1, rows, :].astype(F32)).astype(BF16)
            self.rows_loop(0, half, body)
            self.copy("xa").start()
            def keep(rows, base):
                self.xkeep[base, :] = part[rows, :] + pin[1, rows, :].astype(F32)
            self.rows_loop(half, half, keep)

    def relay_y(self):
        self.copy("xd").wait_recv()
        def body(rows, base):
            self.ysum[rows, :] = (self.ykeep[base, :] + self.xin[base, :].astype(F32)).astype(BF16)
        self.rows_loop(0, self.half, body)
        self.copy("ya").start()

    def relay_x(self):
        self.copy("yd").wait_recv()
        def body(rows, base):
            self.xsum[rows, :] = (self.xkeep[base, :] + self.yin[base, :].astype(F32)).astype(BF16)
        self.rows_loop(self.half, self.half, body)
        self.copy("xb").start()

    def wait_own(self):
        for key in ("p0", "xa", "yb", "ya", "xb"):
            self.copy(key).wait_recv()

    def own(self, rows):
        return (self.part[rows, :] + self.pin[0, rows, :].astype(F32)) + (
            self.ownx[rows, :].astype(F32) + self.owny[rows, :].astype(F32))

    def finish(self):
        for key in self.SENDS:
            self.copy(key).wait_send()


def reduce_scratch(tok, dim):
    half = tok // 2
    return [
        pltpu.VMEM((tok, dim), F32),
        pltpu.VMEM((4, tok, dim), BF16),
        pltpu.VMEM((4, tok, dim), BF16),
        pltpu.VMEM((tok, dim), BF16),
        pltpu.VMEM((tok, dim), BF16),
        pltpu.VMEM((tok, dim), BF16),
        pltpu.VMEM((half, dim), BF16),
        pltpu.VMEM((half, dim), BF16),
        pltpu.VMEM((tok, dim), BF16),
        pltpu.VMEM((tok, dim), BF16),
        pltpu.VMEM((half, dim), F32),
        pltpu.VMEM((half, dim), F32),
        pltpu.SemaphoreType.DMA((10,)),
        pltpu.SemaphoreType.DMA((10,)),
    ]


def comm_params(cid):
    return pltpu.CompilerParams(collective_id=cid, has_side_effects=True, vmem_limit_bytes=VMEM_LIMIT)


def prologue_kernel(cond, cos, sin, b_mod, w_mod, mod_out, cosx_out, sinx_out,
                    wbuf, wsem, mbuf, rbuf, ms, mr, rs, rr):
    nbrs = neighbours()
    me = lax.axis_index("tp")
    blocks, dim, cols = wbuf.shape
    tok, half = cos.shape
    mine = pl.ds(pl.multiple_of(me * cols, cols), cols)
    loads = [pltpu.make_async_copy(w_mod.at[b, :, mine], wbuf.at[b], wsem.at[b]) for b in range(blocks)]
    for load in loads:
        load.start()
    rbuf[0, :, :half] = cos[...]
    rbuf[0, :, half:] = sin[...]
    vec = cond[...].astype(F32)
    silu = (vec * jax.nn.sigmoid(vec)).astype(BF16)
    barrier(nbrs)
    rope = Gather(rbuf, rs, rr, nbrs, 2)
    rope.start_own()
    for b in range(blocks):
        loads[b].wait()
        mbuf[0, b:b + 1, :] = dot(silu, wbuf[b]) + b_mod[b:b + 1, mine].astype(F32)
    mods = Gather(mbuf, ms, mr, nbrs, 1)
    mods.start_own()
    mods.pass_neighbours()
    rope.pass_neighbours()
    mods.pass_diagonal()
    rope.pass_diagonal()
    for slot in (1, 3, 5, 7):
        mods.wait_slot(slot)
        rope.wait_slot(slot)
    for slot in range(8):
        owner = slot_owner(slot)
        mod_out[:, pl.ds(pl.multiple_of(owner * cols, cols), cols)] = mbuf[slot]
    row = lax.broadcasted_iota(jnp.int32, (2 * half, 2 * half), 0)
    lane = lax.broadcasted_iota(jnp.int32, (2 * half, 2 * half), 1)
    pick_cos = jnp.where(row == lax.div(lane, 2), 1.0, 0.0).astype(F32)
    sign = jnp.where(lax.rem(lane, 2) == 0, -1.0, 1.0)
    pick_sin = jnp.where(row == half + lax.div(lane, 2), sign, 0.0).astype(F32)

    def expand(slot, carry):
        both = rbuf[slot]
        cosx_out[slot] = dot(both, pick_cos, precision=lax.Precision.HIGHEST)
        sinx_out[slot] = dot(both, pick_sin, precision=lax.Precision.HIGHEST)
        return carry
    lax.fori_loop(0, 8, expand, 0)
    mods.finish()
    rope.finish()


def prologue(cond, cos, sin, b_mod, w_mod):
    tok, half = cos.shape
    blocks, dim, width = w_mod.shape
    cols = width // 8
    return pl.pallas_call(
        prologue_kernel,
        out_shape=[jax.ShapeDtypeStruct((blocks, width), F32)] + [jax.ShapeDtypeStruct((8, tok, 2 * half), F32)] * 2,
        in_specs=[VM] * 4 + [ANY],
        out_specs=[VM] * 3,
        scratch_shapes=[pltpu.VMEM((blocks, dim, cols), BF16), pltpu.SemaphoreType.DMA((blocks,)),
                        pltpu.VMEM((8, blocks, cols), F32), pltpu.VMEM((8, tok, 2 * half), F32)]
        + gather_sems(1) + gather_sems(2),
        compiler_params=comm_params(0),
        name="prologue",
    )(cond, cos, sin, b_mod, w_mod)


def swap_pairs(tensor):
    lane = lax.broadcasted_iota(jnp.int32, tensor.shape, 1)
    size = tensor.shape[1]
    return jnp.where(lax.rem(lane, 2) == 0, pltpu.roll(tensor, size - 1, 1), pltpu.roll(tensor, 1, 1))


GELU_C = 0.7978845608028654
GELU_A = 0.044715


def gelu(u):
    return 0.5 * u * (1.0 + jnp.tanh(GELU_C * (u + GELU_A * (u * u * u))))


def gelu_grad(u):
    square = u * u
    t = jnp.tanh(GELU_C * (u + GELU_A * (square * u)))
    inner = GELU_C * (1.0 + 3.0 * GELU_A * square)
    return 0.5 * (1.0 + t) + 0.5 * u * (1.0 - t * t) * inner


def layer_norm_rows(x):
    mean = jnp.mean(x, axis=-1, keepdims=True)
    centered = x - mean
    var = jnp.mean(centered * centered, axis=-1, keepdims=True)
    rstd = lax.rsqrt(var + EPS)
    return centered * rstd, rstd


def fwd_in_kernel(blk, x, mod, b_in, qs, ks, cosx, sinx, w_in,
                  h_out, q_out, k_out, v_out, pre_out, u_out, m_out, w_out,
                  hbuf, wraw, wbuf, proj, qst, kst, vst, pst, ust, mst, wsem, osem, hsem, wosem, gs, gr):
    nbrs = neighbours()
    _, tok, dim = hbuf.shape
    cols = b_in.shape[2]
    hd = qs.shape[1]
    loads = dim // 512 if dim >= 512 else 1
    per = dim // loads
    def wload(i):
        rows = pl.ds(i * per, per)
        return pltpu.make_async_copy(w_in.at[blk, rows], wraw.at[rows], wsem.at[i])
    for i in range(loads):
        wload(i).start()
    shift = mod[blk:blk + 1, :dim]
    scale1 = 1.0 + mod[blk:blk + 1, dim:2 * dim]
    def norm(i, carry):
        rows = pl.ds(pl.multiple_of(i * 16, 16), 16)
        normed, _ = layer_norm_rows(x[rows, :].astype(F32))
        hbuf[0, rows, :] = (normed * scale1 + shift).astype(BF16)
        return carry
    lax.fori_loop(0, tok // 16, norm, 0)
    barrier(nbrs)
    gather = Gather(hbuf, gs, gr, nbrs, 4)
    gather.start_own()

    row = lax.broadcasted_iota(jnp.int32, (256, 256), 0)
    lane = lax.broadcasted_iota(jnp.int32, (256, 256), 1)
    pick = jnp.where(lane == 2 * lax.rem(row, 128) + lax.div(row, 128), 1.0, 0.0).astype(BF16)
    for i in range(loads):
        wload(i).wait()
        def split(t, carry, i=i):
            base = pl.multiple_of(i * per + t * 128, 128)
            both = wraw[pl.ds(base, 128)].reshape(256, cols)
            apart = dot(pick, both).astype(BF16)
            wbuf[pl.ds(base, 128), :cols] = apart[:128]
            wbuf[pl.ds(base, 128), cols:] = apart[128:]
            return carry
        lax.fori_loop(0, per // 128, split, 0)
    pltpu.make_async_copy(wbuf, w_out, wosem).start()

    def stores(step, slot):
        return [pltpu.make_async_copy(src.at[slot], dst.at[step], osem.at[slot, j])
                for j, (src, dst) in enumerate(((qst, q_out), (kst, k_out), (vst, v_out), (pst, pre_out), (ust, u_out), (mst, m_out)))]

    def body(step, carry):
        gather.before(step)
        par = lax.rem(step, 2)
        pltpu.make_async_copy(hbuf.at[step], h_out.at[step], hsem.at[step]).start()
        @pl.when(step >= 2)
        def _():
            for cp in stores(step - 2, par):
                cp.wait()
        proj[...] = dot(hbuf[step], wbuf[...])
        def epilogue(i, carry):
            rows = pl.ds(pl.multiple_of(i * 32, 32), 32)
            cx, sx = cosx[step, rows, :], sinx[step, rows, :]
            for head in range(2):
                base = head * cols
                bias = b_in[blk, head:head + 1, :].astype(F32)
                here = pl.ds(head * hd, hd)
                for which, (gain, dst) in enumerate(((qs, qst), (ks, kst))):
                    lanes = which * hd
                    t = proj[rows, base + lanes:base + lanes + hd] + bias[:, lanes:lanes + hd]
                    pst[par, rows, (2 * which + head) * hd:(2 * which + head + 1) * hd] = t
                    n = t * lax.rsqrt(jnp.mean(t * t, axis=-1, keepdims=True) + EPS)
                    n = n * gain[blk:blk + 1, :].astype(F32)
                    dst[par, rows, here] = (n * cx + swap_pairs(n) * sx).astype(BF16)
                vst[par, rows, here] = (proj[rows, base + 2 * hd:base + 3 * hd] + bias[:, 2 * hd:3 * hd]).astype(BF16)
                mlp = cols - 3 * hd
                for j in range(mlp // 128):
                    lo = 3 * hd + j * 128
                    u = proj[rows, base + lo:base + lo + 128] + bias[:, lo:lo + 128]
                    ust[par, rows, head * mlp + j * 128:head * mlp + j * 128 + 128] = u
                    mst[par, rows, head * mlp + j * 128:head * mlp + j * 128 + 128] = gelu(u).astype(BF16)
            return carry
        lax.fori_loop(0, tok // 32, epilogue, 0)
        for cp in stores(step, par):
            cp.start()
        return carry
    lax.fori_loop(0, 8, body, 0)
    for step in (6, 7):
        for cp in stores(step, step % 2):
            cp.wait()
    for step in range(8):
        pltpu.make_async_copy(hbuf.at[step], h_out.at[step], hsem.at[step]).wait()
    pltpu.make_async_copy(wbuf, w_out, wosem).wait()
    gather.finish()


def fwd_in(blk, x, mod, b_in, qs, ks, cosx, sinx, w_in):
    tok, dim = x.shape
    cols = w_in.shape[3]
    hd = qs.shape[1]
    mlp = cols - 3 * hd
    s = jax.ShapeDtypeStruct
    loads = dim // 512 if dim >= 512 else 1
    return pl.pallas_call(
        functools.partial(fwd_in_kernel, blk),
        out_shape=[s((8, tok, dim), BF16)] + [s((8, tok, 2 * hd), BF16)] * 3
        + [s((8, tok, 4 * hd), F32), s((8, tok, 2 * mlp), F32), s((8, tok, 2 * mlp), BF16), s((dim, 2 * cols), BF16)],
        in_specs=[VM] * 7 + [ANY],
        out_specs=[ANY] * 8,
        scratch_shapes=[pltpu.VMEM((8, tok, dim), BF16), pltpu.VMEM((dim, 2, cols), BF16), pltpu.VMEM((dim, 2 * cols), BF16),
                        pltpu.VMEM((tok, 2 * cols), F32)]
        + [pltpu.VMEM((2, tok, 2 * hd), BF16)] * 3
        + [pltpu.VMEM((2, tok, 4 * hd), F32), pltpu.VMEM((2, tok, 2 * mlp), F32), pltpu.VMEM((2, tok, 2 * mlp), BF16)]
        + [pltpu.SemaphoreType.DMA((loads,)), pltpu.SemaphoreType.DMA((2, 6)), pltpu.SemaphoreType.DMA((8,)),
           pltpu.SemaphoreType.DMA] + gather_sems(4),
        compiler_params=comm_params(1 + blk),
        name=f"fwd_in{blk}",
    )(x, mod, b_in, qs, ks, cosx, sinx, w_in)


def fwd_out_kernel(blk, x, mod, b_out, k, v, q, m, w_out, x_new, branch_out, o_out, of_out, lse_out,
                   wbuf, sc, pn, ost, ofst, lst, wsem, osem, *red):
    nbrs = neighbours()
    tok, dim = x.shape
    hd = k.shape[2] // 2
    seq = 8 * tok
    mlp = m.shape[2] // 2
    c2 = LOG2E * hd ** -0.5
    load = pltpu.make_async_copy(w_out.at[blk], wbuf, wsem)
    load.start()
    barrier(nbrs)
    rs = Reduce(*red, nbrs)
    load.wait()

    def stores(slot, par):
        return [pltpu.make_async_copy(src.at[par], dst.at[slot], osem.at[par, j])
                for j, (src, dst) in enumerate(((ost, o_out), (ofst, of_out), (lst, lse_out)))]

    def body(step, carry):
        slot = 7 - step
        par = lax.rem(step, 2)
        @pl.when(step >= 2)
        def _():
            for cp in stores(slot + 2, par):
                cp.wait()
        for head in range(2):
            here = pl.ds(head * hd, hd)
            qh = q[slot, :, here]
            kh = k[:, :, here].reshape(seq, hd)
            sc[...] = dot(qh, kh, ((1,), (1,)))
            vh = v[:, :, here].reshape(seq, hd)
            def soft(i, carry):
                rows = pl.ds(pl.multiple_of(i * 32, 32), 32)
                top = jnp.max(sc[rows, :], axis=-1, keepdims=True) * c2
                e = jnp.exp2(sc[rows, :] * c2 - top)
                total = jnp.sum(e, axis=-1, keepdims=True)
                pn[rows, :] = (e * (1.0 / total)).astype(BF16)
                lst[par, head, rows, :] = jnp.broadcast_to(top + jnp.log2(total), (32, 128))
                return carry
            lax.fori_loop(0, tok // 32, soft, 0)
            o = dot(pn[...], vh)
            ofst[par, :, here] = o
            ost[par, :, here] = o.astype(BF16)
        acc = None
        part = red[0]
        nb = dim // 512 if dim >= 512 else 1
        wd = dim // nb
        for n in range(nb):
            lanes = pl.ds(n * wd, wd)
            acc = None
            for head in range(2):
                t = dot(ost[par, :, head * hd:(head + 1) * hd], wbuf[head, :hd, lanes])
                t = t + dot(m[slot, :, head * mlp:(head + 1) * mlp], wbuf[head, hd:, lanes])
                acc = t if acc is None else acc + t
            part[:, lanes] = acc
        for cp in stores(slot, par):
            cp.start()
        rs.after(step)
        @pl.when(step == 4)
        def _():
            rs.relay_y()
        @pl.when(step == 5)
        def _():
            rs.relay_x()
        return carry
    lax.fori_loop(0, 8, body, 0)
    for slot in (1, 0):
        for cp in stores(slot, (7 - slot) % 2):
            cp.wait()
    rs.wait_own()
    gate = mod[blk:blk + 1, 2 * dim:]
    bias = b_out[blk:blk + 1, :].astype(F32)
    def final(i, carry):
        rows = pl.ds(pl.multiple_of(i * 16, 16), 16)
        branch = rs.own(rows) + bias
        branch_out[rows, :] = branch
        x_new[rows, :] = (x[rows, :].astype(F32) + gate * branch).astype(BF16)
        return carry
    lax.fori_loop(0, tok // 16, final, 0)
    rs.finish()


def fwd_out(blk, x, mod, b_out, k, v, q, m, w_out):
    tok, dim = x.shape
    hd = k.shape[2] // 2
    s = jax.ShapeDtypeStruct
    return pl.pallas_call(
        functools.partial(fwd_out_kernel, blk),
        out_shape=[s((tok, dim), BF16), s((tok, dim), F32), s((8, tok, 2 * hd), BF16), s((8, tok, 2 * hd), F32),
                   s((8, 2, tok, 128), F32)],
        in_specs=[VM] * 7 + [ANY],
        out_specs=[VM] * 2 + [ANY] * 3,
        scratch_shapes=[pltpu.VMEM(w_out.shape[1:], BF16), pltpu.VMEM((tok, 8 * tok), F32), pltpu.VMEM((tok, 8 * tok), BF16),
                        pltpu.VMEM((2, tok, 2 * hd), BF16), pltpu.VMEM((2, tok, 2 * hd), F32), pltpu.VMEM((2, 2, tok, 128), F32),
                        pltpu.SemaphoreType.DMA, pltpu.SemaphoreType.DMA((2, 3))] + reduce_scratch(tok, dim),
        compiler_params=comm_params(3 + blk),
        name=f"fwd_out{blk}",
    )(x, mod, b_out, k, v, q, m, w_out)


def bwd_out_kernel(blk, grad, branch, mod, qs, ks, k, v, q, cosx, sinx, of, lse, pre, u, w_out,
                   db_out, dproj_out, g_bin, d_gate, d_bout, d_qs, d_ks,
                   dbuf, wbuf, dj, dk, dv, dqs, pt, dst, dpst, dkst, ofb, lseb, preb, ub, wsem, isem, osem, ksem, dsem, gs, gr):
    nbrs = neighbours()
    _, tok, dim = dbuf.shape
    hd = qs.shape[1]
    seq = 8 * tok
    mlp = u.shape[2] // 2
    cols = 3 * hd + mlp
    c2 = LOG2E * hd ** -0.5
    load = pltpu.make_async_copy(w_out.at[blk], wbuf, wsem)
    load.start()
    gate = mod[blk:blk + 1, 2 * dim:]

    def fetch(step, par):
        return [pltpu.make_async_copy(src.at[step], dstb.at[par], isem.at[par, j])
                for j, (src, dstb) in enumerate(((of, ofb), (lse, lseb), (pre, preb), (u, ub)))]

    for cp in fetch(0, 0):
        cp.start()

    def head_of(i, carry):
        dgate, dbias = carry
        rows = pl.ds(pl.multiple_of(i * 16, 16), 16)
        g = grad[rows, :].astype(F32)
        gated = g * gate
        dbuf[0, rows, :] = gated.astype(BF16)
        prod = g * branch[rows, :]
        return dgate + prod[:8] + prod[8:], dbias + gated[:8] + gated[8:]
    zero = jnp.zeros((8, dim), F32)
    dgate, dbias = lax.fori_loop(0, tok // 16, head_of, (zero, zero))
    barrier(nbrs)
    gather = Gather(dbuf, gs, gr, nbrs, 4)
    gather.start_own()
    d_gate[...] = jnp.sum(dgate, axis=0, keepdims=True)
    d_bout[...] = jnp.sum(dbias, axis=0, keepdims=True)
    g_bin[...] = jnp.zeros(g_bin.shape, F32)
    d_qs[...] = jnp.zeros(d_qs.shape, F32)
    d_ks[...] = jnp.zeros(d_ks.shape, F32)
    dk[...] = jnp.zeros(dk.shape, F32)
    dv[...] = jnp.zeros(dv.shape, F32)
    load.wait()

    def norm_rope_back(t, dy, cx, sx, gain):
        d = dy * cx - swap_pairs(dy) * sx
        r = lax.rsqrt(jnp.mean(t * t, axis=-1, keepdims=True) + EPS)
        n = t * r
        dn = d * gain
        return r * (dn - n * jnp.mean(dn * n, axis=-1, keepdims=True)), d * n

    def store(step, par):
        return [pltpu.make_async_copy(dpst.at[par], dproj_out.at[step], osem.at[par])]

    def body(step, carry):
        gather.before(step)
        par = lax.rem(step, 2)
        pltpu.make_async_copy(dbuf.at[step], db_out.at[step], dsem.at[step]).start()
        @pl.when(step < 7)
        def _():
            for cp in fetch(step + 1, 1 - par):
                cp.start()
        for head in range(2):
            dj[:, head * (hd + mlp):(head + 1) * (hd + mlp)] = dot(dbuf[step], wbuf[head], ((1,), (1,))).astype(BF16)
        for cp in fetch(step, par):
            cp.wait()
        @pl.when(step >= 2)
        def _():
            for cp in store(step - 2, par):
                cp.wait()
        for head in range(2):
            here = pl.ds(head * hd, hd)
            joined0 = head * (hd + mlp)
            do = dj[:, joined0:joined0 + hd]
            qh = q[step, :, here]
            delta = jnp.sum(jnp.transpose(do.astype(F32) * ofb[par, :, here]), axis=0, keepdims=True)
            lrow = jnp.transpose(lseb[par, head])[:1, :]
            def keys(j, carry):
                kh = k[j, :, here]
                vh = v[j, :, here]
                st = dot(kh, qh, ((1,), (1,)))
                p = jnp.exp2(st * c2 - lrow)
                dp = dot(vh, do, ((1,), (1,)))
                ds = (p * (dp - delta)).astype(BF16)
                dv[j, :, here] += dot(p.astype(BF16), do)
                dk[j, :, here] += dot(ds, qh)
                dst[pl.ds(pl.multiple_of(j * tok, tok), tok), :] = ds
                return carry
            lax.fori_loop(0, 8, keys, 0, unroll=2)
            kh = k[:, :, here].reshape(seq, hd)
            dqs[:, here] = dot(dst[...], kh, ((0,), (0,))) * (hd ** -0.5)

        def epilogue(i, carry):
            rows = pl.ds(pl.multiple_of(i * 32, 32), 32)
            cx, sx = cosx[step, rows, :], sinx[step, rows, :]
            for head in range(2):
                base = head * cols
                t = preb[par, rows, head * hd:(head + 1) * hd]
                gain = qs[blk:blk + 1, :].astype(F32)
                dy = dqs[rows, head * hd:(head + 1) * hd].astype(BF16).astype(F32)
                dt, dg = norm_rope_back(t, dy, cx, sx, gain)
                d_qs[...] += jnp.sum(dg, axis=0, keepdims=True)
                g_bin[:, base:base + hd] += jnp.sum(dt, axis=0, keepdims=True)
                dpst[par, rows, base:base + hd] = dt.astype(BF16)
                dkst[step, rows, head * hd:(head + 1) * hd] = preb[par, rows, (2 + head) * hd:(3 + head) * hd]
                for j in range(mlp // 128):
                    lo = j * 128
                    dm = dj[rows, head * (hd + mlp) + hd + lo:head * (hd + mlp) + hd + lo + 128].astype(F32)
                    du = dm * gelu_grad(ub[par, rows, head * mlp + lo:head * mlp + lo + 128])
                    g_bin[:, base + 3 * hd + lo:base + 3 * hd + lo + 128] += jnp.sum(du, axis=0, keepdims=True)
                    dpst[par, rows, base + 3 * hd + lo:base + 3 * hd + lo + 128] = du.astype(BF16)
            return carry
        lax.fori_loop(0, tok // 32, epilogue, 0)
        for cp in store(step, par):
            cp.start()
        return carry
    lax.fori_loop(0, 8, body, 0)
    for step in (6, 7):
        for cp in store(step, step % 2):
            cp.wait()

    def tail_copies(step, par):
        return [pltpu.make_async_copy(pt.at[par, :, pl.ds(head * 2 * hd, 2 * hd)],
                                      dproj_out.at[step, :, pl.ds(head * cols + hd, 2 * hd)], ksem.at[par, head]) for head in range(2)]

    def tail(step, carry):
        par = lax.rem(step, 2)
        @pl.when(step >= 2)
        def _():
            for cp in tail_copies(step - 2, par):
                cp.wait()
        def rows_of(i, carry):
            rows = pl.ds(pl.multiple_of(i * 32, 32), 32)
            cx, sx = cosx[step, rows, :], sinx[step, rows, :]
            for head in range(2):
                here = slice(head * hd, (head + 1) * hd)
                base = head * cols
                dy = (dk[step, rows, here] * (hd ** -0.5)).astype(BF16).astype(F32)
                dt, dg = norm_rope_back(dkst[step, rows, here], dy, cx, sx, ks[blk:blk + 1, :].astype(F32))
                d_ks[...] += jnp.sum(dg, axis=0, keepdims=True)
                g_bin[:, base + hd:base + 2 * hd] += jnp.sum(dt, axis=0, keepdims=True)
                pt[par, rows, head * 2 * hd:head * 2 * hd + hd] = dt.astype(BF16)
                dvr = dv[step, rows, here].astype(BF16)
                g_bin[:, base + 2 * hd:base + 3 * hd] += jnp.sum(dvr.astype(F32), axis=0, keepdims=True)
                pt[par, rows, head * 2 * hd + hd:(head + 1) * 2 * hd] = dvr
            return carry
        lax.fori_loop(0, tok // 32, rows_of, 0)
        for cp in tail_copies(step, par):
            cp.start()
        return carry
    lax.fori_loop(0, 8, tail, 0)
    for step in (6, 7):
        for cp in tail_copies(step, step % 2):
            cp.wait()
    for step in range(8):
        pltpu.make_async_copy(dbuf.at[step], db_out.at[step], dsem.at[step]).wait()
    gather.finish()


def bwd_out(blk, grad, branch, mod, qs, ks, k, v, q, cosx, sinx, of, lse, pre, u, w_out):
    tok, dim = grad.shape
    hd = qs.shape[1]
    mlp = u.shape[2] // 2
    cols = 3 * hd + mlp
    s = jax.ShapeDtypeStruct
    return pl.pallas_call(
        functools.partial(bwd_out_kernel, blk),
        out_shape=[s((8, tok, dim), BF16), s((8, tok, 2 * cols), BF16), s((1, 2 * cols), F32), s((1, dim), F32), s((1, dim), F32),
                   s((1, hd), F32), s((1, hd), F32)],
        in_specs=[VM] * 10 + [ANY] * 5,
        out_specs=[ANY] * 2 + [VM] * 5,
        scratch_shapes=[pltpu.VMEM((8, tok, dim), BF16), pltpu.VMEM(w_out.shape[1:], BF16), pltpu.VMEM((tok, 2 * (hd + mlp)), BF16),
                        pltpu.VMEM((8, tok, 2 * hd), F32), pltpu.VMEM((8, tok, 2 * hd), F32), pltpu.VMEM((tok, 2 * hd), F32),
                        pltpu.VMEM((2, tok, 4 * hd), BF16), pltpu.VMEM((8 * tok, tok), BF16), pltpu.VMEM((2, tok, 2 * cols), BF16),
                        pltpu.VMEM((8, tok, 2 * hd), F32),
                        pltpu.VMEM((2, tok, 2 * hd), F32), pltpu.VMEM((2, 2, tok, 128), F32), pltpu.VMEM((2, tok, 4 * hd), F32),
                        pltpu.VMEM((2, tok, 2 * mlp), F32),
                        pltpu.SemaphoreType.DMA, pltpu.SemaphoreType.DMA((2, 4)), pltpu.SemaphoreType.DMA((2,)),
                        pltpu.SemaphoreType.DMA((2, 2)), pltpu.SemaphoreType.DMA((8,))] + gather_sems(4),
        compiler_params=comm_params(5 + blk),
        name=f"bwd_out{blk}",
    )(grad, branch, mod, qs, ks, k, v, q, cosx, sinx, of, lse, pre, u, w_out)


def bwd_in_kernel(blk, grad, x, mod, dproj, w, g_new, d_shift, d_scale, wbuf, dbuf, wsem, dsem, *red):
    nbrs = neighbours()
    tok, dim = x.shape
    load = pltpu.make_async_copy(w, wbuf, wsem)
    load.start()
    def fetch(step):
        return pltpu.make_async_copy(dproj.at[7 - step], dbuf.at[step], dsem.at[step])
    for step in range(8):
        fetch(step).start()
    barrier(nbrs)
    rs = Reduce(*red, nbrs)
    load.wait()
    part = red[0]

    def body(step, carry):
        fetch(step).wait()
        part[...] = dot(dbuf[step], wbuf[...], ((1,), (1,)))
        rs.after(step)
        return carry
    lax.fori_loop(0, 8, body, 0)
    rs.relay_y()
    rs.relay_x()
    rs.wait_own()
    scale1 = 1.0 + mod[blk:blk + 1, dim:2 * dim]
    def final(i, carry):
        dshift, dscale = carry
        rows = pl.ds(pl.multiple_of(i * 16, 16), 16)
        nh, rstd = layer_norm_rows(x[rows, :].astype(F32))
        dh = rs.own(rows).astype(BF16).astype(F32)
        dn = dh * scale1
        prod = dh * nh
        dx = rstd * (dn - jnp.mean(dn, axis=-1, keepdims=True) - nh * jnp.mean(dn * nh, axis=-1, keepdims=True))
        g_new[rows, :] = (grad[rows, :].astype(F32) + dx).astype(BF16)
        return dshift + dh[:8] + dh[8:], dscale + prod[:8] + prod[8:]
    zero = jnp.zeros((8, dim), F32)
    dshift, dscale = lax.fori_loop(0, tok // 16, final, (zero, zero))
    d_shift[...] = jnp.sum(dshift, axis=0, keepdims=True)
    d_scale[...] = jnp.sum(dscale, axis=0, keepdims=True)
    rs.finish()


def bwd_in(blk, grad, x, mod, dproj, w):
    tok, dim = x.shape
    s = jax.ShapeDtypeStruct
    return pl.pallas_call(
        functools.partial(bwd_in_kernel, blk),
        out_shape=[s((tok, dim), BF16), s((1, dim), F32), s((1, dim), F32)],
        in_specs=[VM] * 3 + [ANY] * 2,
        out_specs=[VM] * 3,
        scratch_shapes=[pltpu.VMEM(w.shape, BF16), pltpu.VMEM(dproj.shape, BF16), pltpu.SemaphoreType.DMA,
                        pltpu.SemaphoreType.DMA((8,))] + reduce_scratch(tok, dim),
        compiler_params=comm_params(7 + blk),
        name=f"bwd_in{blk}",
    )(grad, x, mod, dproj, w)


def grad_win_kernel(h, dproj, *rest):
    out, stage = rest[-2], rest[-1]
    seq, tile = h.shape
    cols = dproj.shape[1] // 2
    row = lax.broadcasted_iota(jnp.int32, (256, 256), 0)
    lane = lax.broadcasted_iota(jnp.int32, (256, 256), 1)
    join = jnp.where(row == 2 * lax.rem(lane, 128) + lax.div(lane, 128), 1.0, 0.0).astype(BF16)
    stage[...] = dot(h[...], dproj[...], ((0,), (0,))).astype(BF16)
    for t in range(tile // 128):
        rows = slice(t * 128, (t + 1) * 128)
        both = jnp.concatenate([stage[rows, :cols], stage[rows, cols:]], axis=0)
        mixed = dot(join, both).astype(BF16)
        out[0, pl.ds(t * 128, 128)] = mixed.reshape(128, 2, cols)


def grad_win(blk, h, dproj, prev):
    seq = h.shape[0] * h.shape[1]
    dim = h.shape[2]
    width = dproj.shape[2]
    cols = width // 2
    tile = 256
    h2, dp2 = h.reshape(seq, dim), dproj.reshape(seq, width)
    args = [h2, dp2] + ([] if prev is None else [prev])
    return pl.pallas_call(
        grad_win_kernel,
        grid=(dim // tile,),
        out_shape=jax.ShapeDtypeStruct((2, dim, 2, cols), BF16),
        in_specs=[pl.BlockSpec((seq, tile), lambda i: (0, i)), VM] + ([] if prev is None else [ANY]),
        out_specs=pl.BlockSpec((1, tile, 2, cols), lambda i: (blk, i, 0, 0)),
        scratch_shapes=[pltpu.VMEM((tile, width), BF16)],
        input_output_aliases={} if prev is None else {2: 0},
        compiler_params=pltpu.CompilerParams(vmem_limit_bytes=VMEM_LIMIT),
        cost_estimate=pl.CostEstimate(flops=2 * seq * dim * width, bytes_accessed=2 * (seq * (dim + width) + dim * width), transcendentals=0),
        name=f"grad_win{blk}",
    )(*args)


def grad_wout_kernel(o, m, db, *rest):
    out = rest[-1]
    hd = o.shape[1] // 2
    mlp = m.shape[1] // 2
    for head in range(2):
        out[0, head, :hd, :] = dot(o[:, head * hd:(head + 1) * hd], db[...], ((0,), (0,))).astype(BF16)
        out[0, head, hd:, :] = dot(m[:, head * mlp:(head + 1) * mlp], db[...], ((0,), (0,))).astype(BF16)


def grad_wout(blk, o, m, db, prev):
    seq = o.shape[0] * o.shape[1]
    dim = db.shape[2]
    hd, mlp = o.shape[2] // 2, m.shape[2] // 2
    tile = min(256, dim)
    args = [o.reshape(seq, 2 * hd), m.reshape(seq, 2 * mlp), db.reshape(seq, dim)] + ([] if prev is None else [prev])
    return pl.pallas_call(
        grad_wout_kernel,
        grid=(dim // tile,),
        out_shape=jax.ShapeDtypeStruct((2, 2, hd + mlp, dim), BF16),
        in_specs=[VM, VM, pl.BlockSpec((seq, tile), lambda i: (0, i))] + ([] if prev is None else [ANY]),
        out_specs=pl.BlockSpec((1, 2, hd + mlp, tile), lambda i: (blk, 0, 0, i)),
        input_output_aliases={} if prev is None else {3: 0},
        compiler_params=pltpu.CompilerParams(vmem_limit_bytes=VMEM_LIMIT),
        cost_estimate=pl.CostEstimate(flops=4 * seq * dim * (hd + mlp), bytes_accessed=2 * seq * (dim + 2 * hd + 2 * mlp), transcendentals=0),
        name=f"grad_wout{blk}",
    )(*args)


def small_sum_kernel(vec, out, buf, gs, gr):
    nbrs = neighbours()
    buf[0] = vec[...]
    barrier(nbrs)
    gather = Gather(buf, gs, gr, nbrs, 1)
    gather.all_now()
    me = lax.axis_index("tp")
    core, xbit, ybit = lax.rem(me, 2), lax.rem(lax.div(me, 2), 2), lax.div(me, 4)
    total = None
    for owner in range(8):
        oc, ox, oy = owner % 2, (owner // 2) % 2, owner // 4
        slot = (core + oc - 2 * core * oc) + 2 * (xbit + ox - 2 * xbit * ox) + 4 * (ybit + oy - 2 * ybit * oy)
        total = buf[slot] if total is None else total + buf[slot]
    out[...] = total
    gather.finish()


def small_sum(vec):
    return pl.pallas_call(
        small_sum_kernel,
        out_shape=jax.ShapeDtypeStruct(vec.shape, F32),
        in_specs=[VM],
        out_specs=VM,
        scratch_shapes=[pltpu.VMEM((8,) + vec.shape, F32)] + gather_sems(1),
        compiler_params=comm_params(9),
        name="small_sum",
    )(vec)


def solution(mesh):
    act = P("dp", "tp", None)
    in_specs = (act, P("dp", None), P("tp", None), P("tp", None), P(None, None, None), P(None, None), P(None, None, "tp", None), P(None, "tp", None), P(None, None), P(None, None), P(None, "tp", None, None), P(None, None), act)
    out_specs = (act, act, P("dp", None, None), P("dp", None), P("dp", None, "tp", None), P("dp", "tp", None), P("dp", None), P("dp", None), P("dp", "tp", None, None), P("dp", None))

    def device_fn(x_in, cond_vec, rope_cos, rope_sin, w_mod, b_mod, w_in, b_in, q_scale, k_scale, w_out, b_out, d_out):
        blocks = w_in.shape[0]
        dim = x_in.shape[2]
        hd = q_scale.shape[1]
        mod, cosx, sinx = prologue(cond_vec, rope_cos, rope_sin, b_mod, w_mod)
        x = x_in[0]
        saved = []
        for blk in range(blocks):
            h, q, k, v, pre, u, m, w = fwd_in(blk, x, mod, b_in, q_scale, k_scale, cosx, sinx, w_in)
            x_new, branch, o, of, lse = fwd_out(blk, x, mod, b_out, k, v, q, m, w_out)
            saved.append((x, h, q, k, v, pre, u, m, w, branch, o, of, lse))
            x = x_new
        grad = d_out[0]
        gwin = gwout = None
        small, gbin = {}, {}
        for blk in reversed(range(blocks)):
            xb, h, q, k, v, pre, u, m, w, branch, o, of, lse = saved[blk]
            db, dproj, gb, d_gate, d_bout, d_qs, d_ks = bwd_out(blk, grad, branch, mod, q_scale, k_scale, k, v, q, cosx, sinx, of, lse, pre, u, w_out)
            grad, d_shift, d_scale = bwd_in(blk, grad, xb, mod, dproj, w)
            gwin = grad_win(blk, h, dproj, gwin)
            gwout = grad_wout(blk, o, m, db, gwout)
            small[blk] = jnp.concatenate([d_shift, d_scale, d_gate, d_bout, d_qs, d_ks], axis=1)
            gbin[blk] = gb
        sums = small_sum(jnp.concatenate([small[blk] for blk in range(blocks)], axis=0))
        d_mod = sums[:, :3 * dim]
        vec = cond_vec.astype(F32)
        silu = jax.nn.silu(vec).astype(BF16).astype(F32)
        g_wmod = silu[0][None, :, None] * d_mod[:, None, :]
        g_bin = jnp.stack([gbin[blk].reshape(2, -1) for blk in range(blocks)])
        return (x[None], grad[None], g_wmod, d_mod, gwin, g_bin, sums[:, 4 * dim:4 * dim + hd], sums[:, 4 * dim + hd:],
                gwout, sums[:, 3 * dim:4 * dim])

    return jax.shard_map(device_fn, mesh=mesh, in_specs=in_specs, out_specs=out_specs, check_vma=False)
```

time: 1270 us -> 737 us (0.58)
  Pallas kernels: 0 us -> 692 us
  matrix products: 431 us -> 0 us
  waiting for transfers between devices: 325 us -> 0 us
  local copies, waits for them, and re-layouts: 224 us -> 10 us
  other arithmetic: 239 us -> 33.9 us
  blocking collectives: 26.4 us -> 0 us
  between operations: 15.5 us -> 0.94 us
    pallas_call x0 -> x14, Pallas kernels: none -> 692 us  [the longest x2 204 us: bwd_out(): pl.pallas_call(functools.partial(bwd_out_kernel, blk), out_shape=[s((8, t...]
    dot_general x24 -> x0, matrix products: 396 us -> none  [the longest x6 74.2 us: mix_heads(): jnp.einsum('bhqk,bkhe->bqhe', attn_probs, v_part, preferred_element_type=...]
    unnamed x213 -> x44, local copies, waits for them, and re-layouts: 193 us -> 6.65 us
    reduce_scatter x4 -> x0, waiting for transfers between devices: 171 us -> none  [the longest x2 126 us: device_fn(): lax.psum_scatter(part_out.astype(jnp.bfloat16), 'tp', scatter_dimension=1...]
    another operation x16 -> x1, other arithmetic: 133 us -> 0.61 us  [device_fn(): g_bin = jnp.stack([gbin[blk].reshape(2, -1) for blk in range(blocks)])]
    all_gather x4 -> x0, waiting for transfers between devices: 102 us -> none  [the longest x2 60.4 us: device_fn(): lax.all_gather(gated_grad.astype(jnp.bfloat16), 'tp', axis=1, tiled=True)]
    psum x1 -> x0, waiting for transfers between devices: 52.3 us -> none  [device_fn(): d_mod = lax.psum(jnp.concatenate([d_shift, d_scale, d_gate], axis=-1), 'tp')]
    reduce_sum x15 -> x0, other arithmetic: 37.1 us -> none  [the longest x2 10.7 us: mix_heads(): rms_norm(projected[..., head_dim:2 * head_dim]) * k_scale]
  transfers between devices with their start and end apart: 9 -> 0, of which waited for: 8 -> 0; matrix products, arithmetic and copies ran while one was open for 29% -> 0% of each run, Pallas kernels for 0% -> 0%
where the time goes in v1:
time: 737 us
  Pallas kernels  692 us (94%)
  other arithmetic  33.9 us (5%)
  local copies, waits for them, and re-layouts  10 us (1%)
    pallas_call x2, Pallas kernels, bwd_out(): pl.pallas_call(functools.partial(bwd_out_kernel, blk), out_shape=[s((8, t...  204 us
    pallas_call x2, Pallas kernels, fwd_out(): pl.pallas_call(functools.partial(fwd_out_kernel, blk), out_shape=[s((tok,...  151 us
    pallas_call x2, Pallas kernels, fwd_in(): pl.pallas_call(functools.partial(fwd_in_kernel, blk), out_shape=[s((8, to...  114 us
    pallas_call x2, Pallas kernels, bwd_in(): pl.pallas_call(functools.partial(bwd_in_kernel, blk), out_shape=[s((tok,...  108 us
    pallas_call x2, Pallas kernels, grad_win(): pl.pallas_call(grad_win_kernel, grid=(dim // tile,), out_shape=jax.ShapeD...  55.6 us
    pallas_call x2, Pallas kernels, grad_wout(): pl.pallas_call(grad_wout_kernel, grid=(dim // tile,), out_shape=jax.Shape...  33.2 us
    mul x2, other arithmetic, device_fn(): g_wmod = silu[0][None, :, None] * d_mod[:, None, :]  32.5 us
    pallas_call x1, Pallas kernels, prologue(): pl.pallas_call(prologue_kernel, out_shape=[jax.ShapeDtypeStruct((blocks,...  17.7 us

profile of v1, /device:TPU:0, one launch (start us, length us, event | category | flops | bytes accessed | tf_op | source)
XLA Modules:
  0.0 736.7 jit_solution(2188638243603890264)
XLA Ops:
  0.6 0.7 convert_convert_fusion
  1.4 1.6 copy.25.cos
  3.0 1.6 copy.26.sin
  4.6 17.7 %prologue.1 = (f32[2,6144]{1,0:T(2,128)}, f32[8,256,128]{2,1,0:T(8,128)}, f32[8,256,128]{2,1,0:T(8,128)}) custom-call(bf16[1,2048]{1,0:T(2,128)(2,1)} %cond.1, f32[256,64]{1,0:T(8,128)} %copy.25.cos, f32[256,64]{1,0:T(8,128)} %copy.26.sin, bf16[2,6144]{1,0:T(2,128)(2,1)} %b_mod.1, bf16[2,2048,6144]{2,1,0:T(8,128)(2,1)} %w_mod.1), custom_call_target="tpu_custom_call" | custom-call | tf_op jit(solution)/shard_map/prologue/pallas_call | solution.py:337
  22.3 56.7 %fwd_in0.1 = (bf16[8,256,2048]{2,1,0:T(8,128)(2,1)}, bf16[8,256,256]{2,1,0:T(8,128)(2,1)}, bf16[8,256,256]{2,1,0:T(8,128)(2,1)}, bf16[8,256,256]{2,1,0:T(8,128)(...) custom-call(bf16[256,2048]{1,0:T(8,128)(2,1)} %bitcast.15, ...), custom_call_target="tpu_custom_call" | custom-call | tf_op jit(solution)/shard_map/fwd_in0/pallas_call | solution.py:476
  78.9 75.6 %fwd_out0.1 = (bf16[256,2048]{1,0:T(8,128)(2,1)}, f32[256,2048]{1,0:T(8,128)}, bf16[8,256,256]{2,1,0:T(8,128)(2,1)}, f32[8,256,256]{2,1,0:T(8,128)}, f32[8,2,256,128]{3,2,1,0:T(8,128)}) custom-call(bf16[256,2048]{1,0:T(8,128)(2,1)} %bitcast.16, f32[2,6144]{1,0:T(2,128)} %get-tuple-element.59.mod, bf16[2,2048]{1,0:T(2,128)(2,1)} %b_out.3, ...), custom_call_target="tpu_custom_call" | custom-call | tf_op jit(solution)/shard_map/fwd_out0/pallas_call | solution.py:579
  154.6 57.0 %fwd_in1.1 = (bf16[8,256,2048]{2,1,0:T(8,128)(2,1)}, bf16[8,256,256]{2,1,0:T(8,128)(2,1)}, bf16[8,256,256]{2,1,0:T(8,128)(2,1)}, bf16[8,256,256]{2,1,0:T(8,128)(...) custom-call(bf16[256,2048]{1,0:T(8,128)(2,1)} %get-tuple-element.66., ...), custom_call_target="tpu_custom_call" | custom-call | tf_op jit(solution)/shard_map/fwd_in1/pallas_call | solution.py:476
  211.6 75.0 %fwd_out1.1 = (bf16[256,2048]{1,0:T(8,128)(2,1)}, f32[256,2048]{1,0:T(8,128)}, bf16[8,256,256]{2,1,0:T(8,128)(2,1)}, f32[8,256,256]{2,1,0:T(8,128)}, f32[8,2,256,128]{3,2,1,0:T(8,128)}) custom-call(bf16[256,2048]{1,0:T(8,128)(2,1)} %get-tuple-element.66.x, f32[2,6144]{1,0:T(2,128)} %get-tuple-element.59.mod, bf16[2,2048]{1,0:T(2,128)(2,1)} %b_out.3, ...), custom_call_target="tpu_custom_call" | custom-call | tf_op jit(solution)/shard_map/fwd_out1/pallas_call | solution.py:579
  286.6 101.9 %bwd_out1.1 = (bf16[8,256,2048]{2,1,0:T(8,128)(2,1)}, bf16[8,256,1792]{2,1,0:T(8,128)(2,1)}, f32[1,1792]{1,0:T(1,128)}, f32[1,2048]{1,0:T(1,128)}, f32[1,2048]{1...) custom-call(bf16[256,2048]{1,0:T(8,128)(2,1)} %bitcast.22, f32[256,2048]{1,0:T(8,128)} %get-tuple-element.72.branch, ...), custom_call_target="tpu_custom_call" | custom-call | tf_op jit(solution)/shard_map/bwd_out1/pallas_call | solution.py:757
  388.5 53.3 %bwd_in1.1 = (bf16[256,2048]{1,0:T(8,128)(2,1)}, f32[1,2048]{1,0:T(1,128)}, f32[1,2048]{1,0:T(1,128)}) custom-call(bf16[256,2048]{1,0:T(8,128)(2,1)} %bitcast.23, bf16[256,2048]{1,0:T(8,128)(2,1)} %get-tuple-element.66.x, f32[2,6144]{1,0:T(2,128)} %get-tuple-element.59.mod, bf16[8,256,1792]{2,1,0:T(8,128)(2,1)} %get-tuple-element.77.dproj, ...), custom_call_target="tpu_custom_call" | custom-call | tf_op jit(solution)/shard_map/bwd_in1/pallas_call | solution.py:820
  441.7 101.9 %bwd_out0.1 = (bf16[8,256,2048]{2,1,0:T(8,128)(2,1)}, bf16[8,256,1792]{2,1,0:T(8,128)(2,1)}, f32[1,1792]{1,0:T(1,128)}, f32[1,2048]{1,0:T(1,128)}, f32[1,2048]{1...) custom-call(bf16[256,2048]{1,0:T(8,128)(2,1)} %get-tuple-element.79.grad, f32[256,2048]{1,0:T(8,128)} %get-tuple-element.80.branch, ...), custom_call_target="tpu_custom_call" | custom-call | tf_op jit(solution)/shard_map/bwd_out0/pallas_call | solution.py:757
  543.7 54.3 %bwd_in0.1 = (bf16[256,2048]{1,0:T(8,128)(2,1)}, f32[1,2048]{1,0:T(1,128)}, f32[1,2048]{1,0:T(1,128)}) custom-call(bf16[256,2048]{1,0:T(8,128)(2,1)} %get-tuple-element.79.grad, bf16[256,2048]{1,0:T(8,128)(2,1)} %bitcast.17, f32[2,6144]{1,0:T(2,128)} %get-tuple-element.59.mod, bf16[8,256,1792]{2,1,0:T(8,128)(2,1)} %get-tuple-element.85.dproj, ...), custom_call_target="tpu_custom_call" | custom-call | tf_op jit(solution)/shard_map/bwd_in0/pallas_call | solution.py:820
  599.6 0.7 constant_dynamic-update-slice_fusion.4
  601.0 9.6 %small_sum.1 = f32[2,8448]{1,0:T(2,128)} custom-call(f32[2,8448]{1,0:T(2,128)} %pad_maximum_fusion.vec), custom_call_target="tpu_custom_call" | custom-call | tf_op jit(solution)/shard_map/small_sum/pallas_call | solution.py:915
  610.7 1.2 fusion
  611.9 1.3 slice.15
  613.2 0.8 slice.12
  614.0 16.6 %grad_wout1.1.rest_0_ = bf16[2,2,640,2048]{3,2,1,0:T(8,128)(2,1)} custom-call(bf16[2048,256]{1,0:T(8,128)(2,1)} %bitcast.32, bf16[2048,1024]{1,0:T(8,128)(2,1)} %bitcast.21, bf16[2048,2048]{1,0:T(8,128)(2,1)} %bitcast.29), custom_call_target="tpu_custom_call" | custom-call | flops 10737418240 | bytes 13631488 | tf_op jit(solution)/shard_map/grad_wout1/pallas_call | solution.py:884
  630.7 16.6 %grad_wout0.1 = bf16[2,2,640,2048]{3,2,1,0:T(8,128)(2,1)} custom-call(bf16[2048,256]{1,0:T(8,128)(2,1)} %bitcast.31, bf16[2048,1024]{1,0:T(8,128)(2,1)} %bitcast.20, bf16[2048,2048]{1,0:T(8,128)(2,1)} %bitcast.30, bf16[2,2,640,2048]{3,2,1,0:T(8,128)(2,1)} %grad_wout1.1.rest_0_), custom_call_target="tpu_custom_call", output_to_operand_aliasing={{}: (3, {})} | custom-call | flops 10737418240 | bytes 13631488 | tf_op jit(solution)/shard_map/grad_wout0/pallas_call | solution.py:884
  647.3 27.8 %grad_win1.1.rest_0_ = bf16[2,2048,2,896]{3,2,1,0:T(2,128)(2,1)} custom-call(bf16[2048,2048]{1,0:T(8,128)(2,1)} %bitcast.28, bf16[2048,1792]{1,0:T(8,128)(2,1)} %bitcast.18), custom_call_target="tpu_custom_call" | custom-call | flops 15032385536 | bytes 23068672 | tf_op jit(solution)/shard_map/grad_win1/pallas_call | solution.py:855
  675.1 27.8 %grad_win0.1 = bf16[2,2048,2,896]{3,2,1,0:T(2,128)(2,1)} custom-call(bf16[2048,2048]{1,0:T(8,128)(2,1)} %bitcast.27, bf16[2048,1792]{1,0:T(8,128)(2,1)} %bitcast.19, bf16[2,2048,2,896]{3,2,1,0:T(2,128)(2,1)} %grad_win1.1.rest_0_), custom_call_target="tpu_custom_call", output_to_operand_aliasing={{}: (2, {})} | custom-call | flops 15032385536 | bytes 23068672 | tf_op jit(solution)/shard_map/grad_win0/pallas_call | solution.py:855
  702.9 31.8 %broadcast_multiply_fusion = f32[2,2048,6144]{2,1,0:T(8,128)} fusion(f32[2,6144]{1,0:T(2,128)S(1)} %slice.12, f32[2048]{0:T(1024)S(1)} %bitcast.26), kind=kLoop, calls=%fused_computation | loop fusion | flops 25165824 | bytes 100720640 | tf_op jit(solution)/shard_map/mul | solution.py:958
  734.7 1.0 copy.41
  735.7 1.0 copy.42
  (46 shorter events, 2.2 us)
Async XLA Ops:
  543.6 54.5 %copy-start.9 = (f32[1,1792]{1,0:T(1,128)S(1)}, f32[1,1792]{1,0:T(1,128)}, u32[]{:S(2)}) copy-start(f32[1,1792]{1,0:T(1,128)} %get-tuple-element.103) | copy-start | bytes 21508
  543.6 54.5 %copy-start.10 = (f32[1,1792]{1,0:T(1,128)S(1)}, f32[1,1792]{1,0:T(1,128)}, u32[]{:S(2)}) copy-start(f32[1,1792]{1,0:T(1,128)} %get-tuple-element.102) | copy-start | bytes 21508
  543.6 55.2 %copy-start.8 = (f32[1,2048]{1,0:T(1,128)S(1)}, f32[1,2048]{1,0:T(1,128)}, u32[]{:S(2)}) copy-start(f32[1,2048]{1,0:T(1,128)} %get-tuple-element.94) | copy-start | bytes 24580
  543.6 55.2 %copy-start.7 = (f32[1,2048]{1,0:T(1,128)S(1)}, f32[1,2048]{1,0:T(1,128)}, u32[]{:S(2)}) copy-start(f32[1,2048]{1,0:T(1,128)} %get-tuple-element.95) | copy-start | bytes 24580
  543.6 55.2 %copy-start.4 = (f32[1,2048]{1,0:T(1,128)S(1)}, f32[1,2048]{1,0:T(1,128)}, u32[]{:S(2)}) copy-start(f32[1,2048]{1,0:T(1,128)} %get-tuple-element.96) | copy-start | bytes 24580
  543.6 55.2 %copy-start.3 = (f32[1,2048]{1,0:T(1,128)S(1)}, f32[1,2048]{1,0:T(1,128)}, u32[]{:S(2)}) copy-start(f32[1,2048]{1,0:T(1,128)} %get-tuple-element.97) | copy-start | bytes 24580
  543.7 55.2 %copy-start.13 = (f32[1,128]{1,0:T(1,128)S(1)}, f32[1,128]{1,0:T(1,128)}, u32[]{:S(2)}) copy-start(f32[1,128]{1,0:T(1,128)} %get-tuple-element.98) | copy-start | bytes 1540
  543.7 56.6 %copy-start.6 = (f32[1,2048]{1,0:T(1,128)S(1)}, f32[1,2048]{1,0:T(1,128)}, u32[]{:S(2)}) copy-start(f32[1,2048]{1,0:T(1,128)} %get-tuple-element.90) | copy-start | bytes 24580
  543.7 56.6 %copy-start.5 = (f32[1,2048]{1,0:T(1,128)S(1)}, f32[1,2048]{1,0:T(1,128)}, u32[]{:S(2)}) copy-start(f32[1,2048]{1,0:T(1,128)} %get-tuple-element.91) | copy-start | bytes 24580
  543.7 56.6 %copy-start.14 = (f32[1,128]{1,0:T(1,128)S(1)}, f32[1,128]{1,0:T(1,128)}, u32[]{:S(2)}) copy-start(f32[1,128]{1,0:T(1,128)} %get-tuple-element.92) | copy-start | bytes 1540
  543.7 56.6 %copy-start.11 = (f32[1,128]{1,0:T(1,128)S(1)}, f32[1,128]{1,0:T(1,128)}, u32[]{:S(2)}) copy-start(f32[1,128]{1,0:T(1,128)} %get-tuple-element.99) | copy-start | bytes 1540
  543.7 56.6 %copy-start.12 = (f32[1,128]{1,0:T(1,128)S(1)}, f32[1,128]{1,0:T(1,128)}, u32[]{:S(2)}) copy-start(f32[1,128]{1,0:T(1,128)} %get-tuple-element.93) | copy-start | bytes 1540
  614.0 88.9 %copy-start.2 = (f32[2,6144]{1,0:T(2,128)}, f32[2,6144]{1,0:T(2,128)S(1)}, u32[]{:S(2)}) copy-start(f32[2,6144]{1,0:T(2,128)S(1)} %slice.12) | copy-start | bytes 147460
  702.9 31.8 %copy-start = (bf16[256,2048]{1,0:T(8,128)(2,1)S(1)}, bf16[256,2048]{1,0:T(8,128)(2,1)}, u32[]{:S(2)}) copy-start(bf16[256,2048]{1,0:T(8,128)(2,1)} %get-tuple-element.71) | copy-start | bytes 3145732
  702.9 32.8 %copy-start.1 = (bf16[256,2048]{1,0:T(8,128)(2,1)S(1)}, bf16[256,2048]{1,0:T(8,128)(2,1)}, u32[]{:S(2)}) copy-start(bf16[256,2048]{1,0:T(8,128)(2,1)} %get-tuple-element.87) | copy-start | bytes 3145732
